TPU v7x, 32 devices: a whole 2x2x4 slice. The times are simulated.
32 devices in a mesh: src: 8 (over z, core), cand: 4 (over y, x).
Axes of the slice: x: 2, y: 2, z: 4, core: 2. Of those that a mesh axis runs over, the one named last changes fastest.
Arguments:
- layer_input: bfloat16 [32, 128, 1024], P(('src', 'cand')), parts along dimension 0, may hold values from -16 to 16
- token_ids: int32 [32, 128], P(('src', 'cand')), parts along dimension 0, may hold values from 0 to 50264
- lengths: int32 [32], P(('src', 'cand')), parts along dimension 0, may hold values from 32 to 128
- idf_table: float32 [402120], P('src'), parts along dimension 0, may hold values from 1 to 12
- query_weight: bfloat16 [1024, 1024], P('cand'), may hold values from -0.1875 to 0.1875
- key_weight: bfloat16 [1024, 1024], P('cand'), may hold values from -0.1875 to 0.1875
- value_weight: bfloat16 [1024, 1024], P('cand'), may hold values from -0.1875 to 0.1875
- output_weight: bfloat16 [1024, 1024], P('cand'), may hold values from -0.1875 to 0.1875
Outputs:
- embedded: bfloat16 [32, 128, 1024], P(('src', 'cand')), parts along dimension 0
- pair_utility: float32 [32, 4], P(('src', 'cand')), parts along dimension 0
- expected_utility: float32 [32], P(('src', 'cand')), parts along dimension 0
There are 8 independent parts, one for each index of `src`. A program takes and returns all parts, laid end to end along the dimension named above; an argument that names none is the same for every part. Nothing has to cross between parts.
All inputs are finite; a program needn't handle non-finite values.
Results may differ from a plain program's by a relative error of at most 0.0086.
Values may be sent and summed in bfloat16 or wider, within the bound.
A program may use at most 64 MiB of HBM per device.

v0:
```python
import math

import jax
import jax.numpy as jnp
from jax import lax
from jax.sharding import PartitionSpec as P

HEAD = 64


def block_utility(own_vectors, own_weight, far_vectors, far_weight):
    own_count, length, width = own_vectors.shape
    far_count = far_vectors.shape[0]
    similar = lax.dot_general(
        own_vectors.reshape(own_count * length, width),
        far_vectors.reshape(far_count * length, width),
        (((1,), (1,)), ((), ())),
        preferred_element_type=jnp.float32,
    )
    similar = similar.reshape(own_count, length, far_count, length)
    own_usable = own_weight > 0
    far_usable = far_weight > 0
    best_far = jnp.max(jnp.where(far_usable[None, None, :, :], similar, -4.0), axis=3)
    best_own = jnp.max(jnp.where(own_usable[:, :, None, None], similar, -4.0), axis=1)
    own_float = own_weight.astype(jnp.float32)
    far_float = far_weight.astype(jnp.float32)
    forward = jnp.einsum("il,ilj->ij", own_float, best_far, precision=lax.Precision.HIGHEST)
    forward = forward / jnp.sum(own_float, axis=1)[:, None]
    backward = jnp.einsum("jm,ijm->ij", far_float, best_own, precision=lax.Precision.HIGHEST)
    backward = backward / jnp.sum(far_float, axis=1)[None, :]
    return 0.5 * (forward + backward)


def shards(
    layer_input,
    token_ids,
    lengths,
    idf_table,
    query_weight,
    key_weight,
    value_weight,
    output_weight,
):
    local_cands, length, width = layer_input.shape
    cycle_size = lax.axis_size("cand")
    all_cands = local_cands * cycle_size
    head_size = HEAD
    head_count = width // head_size
    flat = layer_input.reshape(local_cands * length, width)
    pieces = (
        lax.all_gather(query_weight, "cand", axis=0, tiled=True),
        lax.all_gather(key_weight, "cand", axis=0, tiled=True),
        lax.all_gather(value_weight, "cand", axis=0, tiled=True),
    )
    columns = flat
    queries, key_rows, value_rows = tuple(
        (jnp.dot(columns, piece, preferred_element_type=jnp.float32) for piece in pieces)
    )
    queries = queries.astype(jnp.bfloat16).reshape(local_cands, length, head_count, head_size)
    key_rows = key_rows.astype(jnp.bfloat16).reshape(local_cands, length, head_count, head_size)
    value_rows = value_rows.astype(jnp.bfloat16).reshape(local_cands, length, head_count, head_size)
    positions = jnp.arange(length, dtype=jnp.int32)
    valid = positions[None, :] < lengths[:, None]
    scale = 1.0 / math.sqrt(head_size)
    scores = (
        jnp.einsum("clhe,cmhe->chlm", queries, key_rows, preferred_element_type=jnp.float32) * scale
    )
    scores = jnp.where(valid[:, None, None, :], scores, -1000000000.0)
    highest = jnp.max(scores, axis=-1, keepdims=True)
    expo = jnp.exp(scores - highest)
    probs = (expo / jnp.sum(expo, axis=-1, keepdims=True)).astype(jnp.bfloat16)
    context = jnp.einsum("chlm,cmhe->clhe", probs, value_rows, preferred_element_type=jnp.float32)
    context = context.astype(jnp.bfloat16).reshape(local_cands * length, width)
    columns = context
    mixed = jnp.dot(
        columns,
        lax.all_gather(output_weight, "cand", axis=0, tiled=True),
        preferred_element_type=jnp.float32,
    ) + flat.astype(jnp.float32)
    centred = mixed - jnp.mean(mixed, axis=-1, keepdims=True)
    squares = jnp.sum(centred * centred, axis=-1, keepdims=True)
    embedded = (
        (centred / jnp.sqrt(squares + 0.001))
        .astype(jnp.bfloat16)
        .reshape(local_cands, length, width)
    )
    token_weight = (jnp.take(idf_table, token_ids, axis=0) * valid.astype(jnp.float32)).astype(
        jnp.bfloat16
    )
    myself = lax.axis_index("cand")
    piece = (
        lax.all_gather(embedded, "cand", axis=0, tiled=True),
        lax.all_gather(token_weight, "cand", axis=0, tiled=True),
    )
    utility = block_utility(embedded, token_weight, piece[0], piece[1])
    blocks = utility.reshape(local_cands, cycle_size, local_cands)
    own_part = lax.dynamic_slice(blocks, (0, myself, 0), (local_cands, 1, local_cands))[:, 0, :]
    diagonal = jnp.diagonal(own_part)
    expected_utility = (jnp.sum(utility, axis=1) - diagonal) / (all_cands - 1)
    return (embedded, utility, expected_utility)


def solution(mesh):
    in_specs = (
        P(("src", "cand"), None, None),
        P(("src", "cand"), None),
        P(("src", "cand")),
        P("src"),
        P("cand", None),
        P("cand", None),
        P("cand", None),
        P("cand", None),
    )
    out_specs = (P(("src", "cand"), None, None), P(("src", "cand"), None), P(("src", "cand")))
    return jax.shard_map(shards, mesh=mesh, in_specs=in_specs, out_specs=out_specs, check_vma=False)
```

profile of v0, /device:TPU:0, one launch (start us, length us, event | category | flops | bytes accessed | tf_op | source)
XLA Modules:
  0.0 202.1 jit_solution(80820484909239252)
XLA Ops:
  7.2 0.7 all-gather.8.cloned.1.call-update
  8.0 0.7 all-gather.10.cloned.1.call-update
  8.7 0.7 all-gather.12.cloned.1.call-update
  9.5 0.5 all-gather.14.cloned.1.call-update
  10.7 37.1 %all-gather.8.cloned.1.call-done = bf16[1024,1024]{1,0:T(8,128)(2,1)} async-done(((bf16[256,1024]{1,0:T(8,128)(2,1)}), bf16[1024,1024]{1,0:T(8,128)(2,1)}) %all-gather.8.cloned.1.call-update) | async-done | bytes 2097168 | tf_op jit(solution)/shard_map/all_gather | solution.py:53
  47.8 2.1 %convolution_convert_fusion.3 = bf16[128,1024]{1,0:T(8,128)(2,1)S(1)} fusion(bf16[1024,1024]{1,0:T(8,128)(2,1)} %all-gather.8.cloned.1.call-done, bf16[1,128,1024]{2,1,0:T(8,128)(2,1)S(1)} %copy-done.1), kind=kOutput, calls=%fused_computation.10 | convolution fusion | flops 268566528 | bytes 2621440 | tf_op jit(solution)/shard_map/dot_general | solution.py:57
  50.0 34.8 %all-gather.10.cloned.1.call-done = bf16[1024,1024]{1,0:T(8,128)(2,1)} async-done(((bf16[256,1024]{1,0:T(8,128)(2,1)}), bf16[1024,1024]{1,0:T(8,128)(2,1)}) %all-gather.10.cloned.1.call-update) | async-done | bytes 2097168 | tf_op jit(solution)/shard_map/all_gather | solution.py:51
  84.8 2.0 %convolution_convert_fusion.2 = bf16[128,1024]{1,0:T(8,128)(2,1)S(1)} fusion(bf16[1024,1024]{1,0:T(8,128)(2,1)} %all-gather.10.cloned.1.call-done, bf16[1,128,1024]{2,1,0:T(8,128)(2,1)S(1)} %copy-done.1), kind=kOutput, calls=%fused_computation.9 | convolution fusion | flops 268566528 | bytes 2621440 | tf_op jit(solution)/shard_map/dot_general | solution.py:57
  87.1 34.8 %all-gather.12.cloned.1.call-done = bf16[1024,1024]{1,0:T(8,128)(2,1)} async-done(((bf16[256,1024]{1,0:T(8,128)(2,1)}), bf16[1024,1024]{1,0:T(8,128)(2,1)}) %all-gather.12.cloned.1.call-update) | async-done | bytes 2097168 | tf_op jit(solution)/shard_map/all_gather | solution.py:52
  121.9 2.0 %convolution_convert_fusion.1 = bf16[128,1024]{1,0:T(8,128)(2,1)S(1)} fusion(bf16[1024,1024]{1,0:T(8,128)(2,1)} %all-gather.12.cloned.1.call-done, bf16[1,128,1024]{2,1,0:T(8,128)(2,1)S(1)} %copy-done.1), kind=kOutput, calls=%fused_computation.8 | convolution fusion | flops 268566528 | bytes 2621440 | tf_op jit(solution)/shard_map/dot_general | solution.py:57
  124.1 0.5 fusion.18
  124.7 0.4 fusion.3
  125.0 0.4 convolution_convert_fusion
  125.4 33.4 %all-gather.14.cloned.1.call-done = bf16[1024,1024]{1,0:T(8,128)(2,1)} async-done(((bf16[256,1024]{1,0:T(8,128)(2,1)}), bf16[1024,1024]{1,0:T(8,128)(2,1)}) %all-gather.14.cloned.1.call-update) | async-done | bytes 2097168 | tf_op jit(solution)/shard_map/all_gather | solution.py:77
  158.8 2.2 %fusion.19 = (f32[128]{0:T(128)S(1)}, f32[128,1024]{1,0:T(8,128)S(1)}) fusion(bf16[1,128,1024]{2,1,0:T(8,128)(2,1)S(1)} %copy-done.1, bf16[128,1024]{0,1:T(8,128)(2,1)S(1)} %bitcast.70, bf16[1024,1024]{1,0:T(8,128)(2,1)} %all-gather.14.cloned.1.call-done), kind=kOutput, calls=%fused_computation.43 | convolution fusion | flops 268828544 | bytes 3146240 | tf_op jit(solution)/shard_map/dot_general | solution.py:75
  161.2 0.9 divide_convert_fusion.1
  162.1 1.1 gather_fusion
  163.3 0.6 convert_reduce_fusion.1
  163.9 7.9 %all-gather.1 = bf16[4,1,128]{2,1,0:T(2,128)(2,1)S(1)} all-gather(bf16[1,1,128]{2,1,0:T(2,128)(2,1)S(1)} %bitcast.71), channel_id=1, replica_groups=mesh['src'=8,'cand'=4] {'cand'}, dimensions={0}, use_global_device_ids=true | all-gather | bytes 1280 | tf_op jit(solution)/shard_map/all_gather | solution.py:93
  171.8 0.8 fusion.35
  172.6 16.1 %all-gather.16.cloned.1.call-done = bf16[512,1024]{1,0:T(8,128)(2,1)} async-done(((bf16[128,1024]{1,0:T(8,128)(2,1)}), bf16[512,1024]{1,0:T(8,128)(2,1)}) %all-gather.16.cloned.1.call-update) | async-done | bytes 1048592 | tf_op jit(solution)/shard_map/all_gather | solution.py:92
  188.7 1.8 select_reduce_fusion
  191.0 1.4 fusion.20
  192.4 0.7 gather.9
  (28 shorter events, 1.4 us)
Async XLA Ops:
  7.2 154.9 %copy-start = (f32[50265]{0:T(1024)S(1)}, f32[50265]{0:T(1024)}, u32[]{:S(2)}) copy-start(f32[50265]{0:T(1024)} %param.11) | copy-start | bytes 603184
  7.2 40.6 %copy-start.1 = (bf16[1,128,1024]{2,1,0:T(8,128)(2,1)S(1)}, bf16[1,128,1024]{2,1,0:T(8,128)(2,1)}, u32[]{:S(2)}) copy-start(bf16[1,128,1024]{2,1,0:T(8,128)(2,1)} %param.8) | copy-start | bytes 786436
  7.2 40.6 %all-gather.8.cloned.1.call-start = ((), (), s32[]{:S(2)}) async-start(), calls=%async_computation | async-start | bytes 2621440 | tf_op jit(solution)/shard_map/all_gather | solution.py:53
  7.9 76.9 %all-gather.10.cloned.1.call-start = ((), (), s32[]{:S(2)}) async-start(), calls=%async_computation.1 | async-start | bytes 2621440 | tf_op jit(solution)/shard_map/all_gather | solution.py:51
  8.7 113.2 %all-gather.12.cloned.1.call-start = ((), (), s32[]{:S(2)}) async-start(), calls=%async_computation.2 | async-start | bytes 2621440 | tf_op jit(solution)/shard_map/all_gather | solution.py:52
  9.4 149.4 %all-gather.14.cloned.1.call-start = ((), (), s32[]{:S(2)}) async-start(), calls=%async_computation.3 | async-start | bytes 2621440 | tf_op jit(solution)/shard_map/all_gather | solution.py:77
  10.0 178.7 %all-gather.16.cloned.1.call-start = ((), (), s32[]{:S(2)}) async-start(), calls=%async_computation.4 | async-start | bytes 1310720 | tf_op jit(solution)/shard_map/all_gather | solution.py:92
  158.8 3.3 %copy-start.3 = (s32[1,128]{1,0:T(1,128)S(1)}, s32[1,128]{1,0:T(1,128)}, u32[]{:S(2)}) copy-start(s32[1,128]{1,0:T(1,128)} %param.9) | copy-start | bytes 1540
  192.4 2.0 copy-start.2
Sparse Core Ops, SparseCore 0:
  9.8 37.8 all-gather.7
  49.6 35.1 all-gather.9
  86.7 35.1 all-gather.11
  123.6 35.1 all-gather.13
  162.2 26.4 all-gather.15
where the time goes:
time: 202 us
  waiting for transfers between devices  159 us (79%)
  between operations  17.1 us (8%)
  matrix products  12.8 us (6%)
  blocking collectives  7.88 us (4%)
  other arithmetic  2.9 us (1%)
  local copies, waits for them, and re-layouts  2.43 us (1%)
    all_gather x1, waiting for transfers between devices, shards(): lax.all_gather(value_weight, 'cand', axis=0, tiled=True)  37.1 us
    all_gather x1, waiting for transfers between devices, shards(): lax.all_gather(key_weight, 'cand', axis=0, tiled=True)  34.8 us
    all_gather x1, waiting for transfers between devices, shards(): lax.all_gather(query_weight, 'cand', axis=0, tiled=True)  34.8 us
    all_gather x1, waiting for transfers between devices, shards(): lax.all_gather(output_weight, 'cand', axis=0, tiled=True)  33.4 us
    all_gather x1, waiting for transfers between devices, shards(): lax.all_gather(embedded, 'cand', axis=0, tiled=True)  16.1 us
    all_gather x1, blocking collectives, shards(): lax.all_gather(token_weight, 'cand', axis=0, tiled=True)  7.88 us
    dot_general x3, matrix products, shards(): jnp.dot(columns, piece, preferred_element_type=jnp.float32)  6.15 us
  transfers between devices with their start and end apart: 5, of which 5 were waited for; matrix products, arithmetic and copies ran while one was open for 5% of the time, Pallas kernels for 0%

commit v1 on v0

--- a/solution.py
+++ b/solution.py
@@ -1,8 +1,11 @@
+import functools
 import math
 
 import jax
 import jax.numpy as jnp
 from jax import lax
+from jax.experimental import pallas as pl
+from jax.experimental.pallas import tpu as pltpu
 from jax.sharding import PartitionSpec as P
 
 HEAD = 64
@@ -31,7 +34,7 @@
     return 0.5 * (forward + backward)
 
 
-def shards(
+def gathered_shards(
     layer_input,
     token_ids,
     lengths,
@@ -100,6 +103,294 @@
     return (embedded, utility, expected_utility)
 
 
+def remote(src_ref, dst_ref, send_sem, recv_sem, device):
+    return pltpu.make_async_remote_copy(
+        src_ref=src_ref,
+        dst_ref=dst_ref,
+        send_sem=send_sem,
+        recv_sem=recv_sem,
+        device_id=device,
+        device_id_type=pl.DeviceIdType.MESH,
+    )
+
+
+def flipped(index, bits):
+    result = index
+    place = 1
+    while place <= bits:
+        if bits & place:
+            digit = lax.rem(lax.div(index, place), 2)
+            result = result + place - 2 * place * digit
+        place *= 2
+    return result
+
+
+def kernel(
+    count,
+    x_hbm,
+    meta_hbm,
+    q_hbm,
+    k_hbm,
+    v_hbm,
+    o_hbm,
+    embedded_hbm,
+    utility_ref,
+    expected_ref,
+    stage,
+    full,
+    out_rows,
+    x_all,
+    meta,
+    part_out,
+    part_in,
+    vectors,
+    local_sem,
+    w_send,
+    w_recv,
+    f_send,
+    f_recv,
+    x_send,
+    x_recv,
+    m_send,
+    m_recv,
+    p_send,
+    p_recv,
+    e_send,
+    e_recv,
+):
+    group, me = lax.axis_index("src"), lax.axis_index("cand")
+    core = lax.rem(group, 2)
+    sibling = (flipped(group, 1), me)
+    others = range(1, count)
+    peer = [(group, flipped(me, bits)) for bits in range(count)]
+    length, width = x_hbm.shape
+    rows, columns = stage.shape[1], full.shape[2]
+    half = rows // 2
+
+    def column_block(index):
+        return pl.ds(pl.multiple_of(index * columns, columns), columns)
+
+    def row_block(index):
+        return pl.ds(pl.multiple_of(index * rows, rows), rows)
+
+    def row_half(index, which):
+        return pl.ds(pl.multiple_of(index * rows + which * half, half), half)
+
+    own_half = pl.ds(pl.multiple_of(core * half, half), half)
+
+    weights = (q_hbm, k_hbm, v_hbm)
+    loads = [pltpu.make_async_copy(w, stage.at[t], local_sem.at[t]) for t, w in enumerate(weights)]
+    loads += [
+        pltpu.make_async_copy(x_hbm, x_all.at[0], local_sem.at[3]),
+        pltpu.make_async_copy(meta_hbm, meta.at[0], local_sem.at[4]),
+    ]
+    loads += [
+        pltpu.make_async_copy(
+            w.at[:, column_block(me)], full.at[t, row_block(me), :], local_sem.at[5 + t]
+        )
+        for t, w in enumerate(weights)
+    ]
+    loads += [pltpu.make_async_copy(o_hbm, out_rows, local_sem.at[8])]
+    for load in loads:
+        load.start()
+
+    barrier = pltpu.get_barrier_semaphore()
+    for target in [sibling] + [peer[r] for r in others]:
+        pl.semaphore_signal(barrier, inc=1, device_id=target, device_id_type=pl.DeviceIdType.MESH)
+    pl.semaphore_wait(barrier, count)
+
+    for t in range(3):
+        loads[t].wait()
+    w_copies, f_copies, x_copies, m_copies = {}, {}, {}, {}
+    for r in others:
+        w_copies[r] = remote(
+            stage.at[:, own_half, column_block(peer[r][1])],
+            full.at[:, row_half(me, core), :],
+            w_send.at[r],
+            w_recv.at[r],
+            peer[r],
+        )
+        w_copies[r].start()
+    loads[3].wait()
+    loads[4].wait()
+    for r in others:
+        m_copies[r] = remote(meta.at[0], meta.at[r], m_send.at[r], m_recv.at[r], peer[r])
+        m_copies[r].start()
+    for r in others:
+        x_copies[r] = remote(x_all.at[0], x_all.at[r], x_send.at[r], x_recv.at[r], peer[r])
+        x_copies[r].start()
+    for r in others:
+        w_copies[r].wait_recv()
+        landed = full.at[:, row_half(peer[r][1], core), :]
+        f_copies[r] = remote(landed, landed, f_send.at[r], f_recv.at[r], sibling)
+        f_copies[r].start()
+    for load in loads[5:]:
+        load.wait()
+    for r in others:
+        f_copies[r].wait_recv()
+
+    lane = lax.broadcasted_iota(jnp.int32, (1, 2 * HEAD), 1)
+    scale = 1.0 / math.sqrt(HEAD)
+    first = (lane < HEAD).astype(jnp.float32)
+    keep = [(first * scale).astype(jnp.bfloat16), ((1.0 - first) * scale).astype(jnp.bfloat16)]
+
+    def partial_of(r):
+        rows_in = x_all[r]
+        queries, key_rows, value_rows = tuple(
+            jnp.dot(rows_in, full[t], preferred_element_type=jnp.float32).astype(jnp.bfloat16)
+            for t in range(3)
+        )
+        valid = meta[r, 1:2, :] > 0.0
+        pieces = []
+        for start in range(0, columns, 2 * HEAD):
+            span = slice(start, start + 2 * HEAD)
+            q_pair, k_pair, v_pair = queries[:, span], key_rows[:, span], value_rows[:, span]
+            stacked = jnp.concatenate([q_pair * keep[0], q_pair * keep[1]], axis=0)
+            scores = lax.dot_general(
+                stacked, k_pair, (((1,), (1,)), ((), ())), preferred_element_type=jnp.float32
+            )
+            scores = jnp.where(valid, scores, -1000000000.0)
+            expo = jnp.exp(scores - jnp.max(scores, axis=-1, keepdims=True))
+            total = jnp.sum(expo, axis=-1, keepdims=True)
+            summed = jnp.dot(
+                expo.astype(jnp.bfloat16), v_pair, preferred_element_type=jnp.float32
+            )
+            summed = summed / total
+            pieces.append(jnp.where(lane < HEAD, summed[:length], summed[length:]))
+        context = jnp.concatenate(pieces, axis=1).astype(jnp.bfloat16)
+        return jnp.dot(context, out_rows[...], preferred_element_type=jnp.float32)
+
+    mixed = partial_of(0) + x_all[0].astype(jnp.float32)
+    p_copies = {}
+    for r in others:
+        x_copies[r].wait_recv()
+        m_copies[r].wait_recv()
+        part_out[r] = partial_of(r).astype(jnp.bfloat16)
+        p_copies[r] = remote(part_out.at[r], part_in.at[r], p_send.at[r], p_recv.at[r], peer[r])
+        p_copies[r].start()
+    for r in others:
+        p_copies[r].wait_recv()
+        mixed = mixed + part_in[r].astype(jnp.float32)
+    centred = mixed - jnp.mean(mixed, axis=-1, keepdims=True)
+    squares = jnp.sum(centred * centred, axis=-1, keepdims=True)
+    own = (centred / jnp.sqrt(squares + 0.001)).astype(jnp.bfloat16)
+    vectors[0] = own
+    e_copies = {}
+    for r in others:
+        e_copies[r] = remote(vectors.at[0], vectors.at[r], e_send.at[r], e_recv.at[r], peer[r])
+        e_copies[r].start()
+    store = pltpu.make_async_copy(vectors.at[0], embedded_hbm, local_sem.at[0])
+    store.start()
+
+    own_weight = meta[0, 0:1, :]
+    own_column = jnp.broadcast_to(own_weight, (length, length)).T
+    own_total = jnp.sum(own_weight, axis=1, keepdims=True)
+    slot = lax.broadcasted_iota(jnp.int32, utility_ref.shape, 1)
+    utility = jnp.zeros(utility_ref.shape, jnp.float32)
+    everything = jnp.zeros((1, 1), jnp.float32)
+    diagonal = None
+    for r in range(count):
+        if r:
+            e_copies[r].wait_recv()
+        far_weight = meta[r, 0:1, :]
+        similar = lax.dot_general(
+            own, vectors[r], (((1,), (1,)), ((), ())), preferred_element_type=jnp.float32
+        )
+        best_far = jnp.max(jnp.where(far_weight > 0, similar, -4.0), axis=1, keepdims=True)
+        best_own = jnp.max(jnp.where(own_column > 0, similar, -4.0), axis=0, keepdims=True)
+        forward = jnp.sum(own_column[:, 0:1] * best_far, axis=0, keepdims=True) / own_total
+        backward = jnp.sum(far_weight * best_own, axis=1, keepdims=True) / jnp.sum(
+            far_weight, axis=1, keepdims=True
+        )
+        pair = 0.5 * (forward + backward)
+        utility = jnp.where(slot == peer[r][1], pair, utility)
+        everything = everything + pair
+        if r == 0:
+            diagonal = pair
+    utility_ref[...] = utility
+    expected_ref[...] = (everything - diagonal) / (count - 1)
+
+    store.wait()
+    for r in others:
+        for copies in (w_copies, f_copies, x_copies, m_copies, p_copies, e_copies):
+            copies[r].wait_send()
+
+
+def shards(
+    sizes,
+    layer_input,
+    token_ids,
+    lengths,
+    idf_table,
+    query_weight,
+    key_weight,
+    value_weight,
+    output_weight,
+):
+    local_cands, length, width = layer_input.shape
+    count = sizes["cand"]
+    rows = query_weight.shape[0]
+    columns = width // count
+    if (
+        local_cands != 1
+        or count < 2
+        or count & (count - 1)
+        or sizes["src"] % 2
+        or columns % (2 * HEAD)
+        or rows % 32
+        or length != 128
+    ):
+        return gathered_shards(
+            layer_input,
+            token_ids,
+            lengths,
+            idf_table,
+            query_weight,
+            key_weight,
+            value_weight,
+            output_weight,
+        )
+    valid = (jnp.arange(length, dtype=jnp.int32)[None, :] < lengths[:, None]).astype(jnp.float32)
+    token_weight = jnp.take(idf_table, token_ids, axis=0) * valid
+    token_weight = token_weight.astype(jnp.bfloat16).astype(jnp.float32)
+    row = lax.broadcasted_iota(jnp.int32, (8, length), 0)
+    meta = jnp.where(row == 0, token_weight, valid)
+    anywhere = pl.BlockSpec(memory_space=pl.ANY)
+    in_vmem = pl.BlockSpec(memory_space=pltpu.VMEM)
+    pairs = pltpu.SemaphoreType.DMA((count,))
+    embedded, utility, expected = pl.pallas_call(
+        functools.partial(kernel, count),
+        out_shape=(
+            jax.ShapeDtypeStruct((length, width), jnp.bfloat16),
+            jax.ShapeDtypeStruct((1, count), jnp.float32),
+            jax.ShapeDtypeStruct((1, 1), jnp.float32),
+        ),
+        in_specs=[anywhere] * 6,
+        out_specs=(anywhere, in_vmem, in_vmem),
+        scratch_shapes=[
+            pltpu.VMEM((3, rows, width), jnp.bfloat16),
+            pltpu.VMEM((3, rows * count, columns), jnp.bfloat16),
+            pltpu.VMEM((rows, width), jnp.bfloat16),
+            pltpu.VMEM((count, length, width), jnp.bfloat16),
+            pltpu.VMEM((count, 8, length), jnp.float32),
+            pltpu.VMEM((count, length, width), jnp.bfloat16),
+            pltpu.VMEM((count, length, width), jnp.bfloat16),
+            pltpu.VMEM((count, length, width), jnp.bfloat16),
+            pltpu.SemaphoreType.DMA((9,)),
+        ]
+        + [pairs] * 12,
+        compiler_params=pltpu.CompilerParams(collective_id=0, has_side_effects=True),
+    )(
+        layer_input.reshape(length, width),
+        meta,
+        query_weight,
+        key_weight,
+        value_weight,
+        output_weight,
+    )
+    return (embedded.reshape(1, length, width), utility, expected.reshape(1))
+
+
 def solution(mesh):
     in_specs = (
         P(("src", "cand"), None, None),
@@ -112,4 +403,10 @@
         P("cand", None),
     )
     out_specs = (P(("src", "cand"), None, None), P(("src", "cand"), None), P(("src", "cand")))
-    return jax.shard_map(shards, mesh=mesh, in_specs=in_specs, out_specs=out_specs, check_vma=False)
+    return jax.shard_map(
+        functools.partial(shards, dict(mesh.shape)),
+        mesh=mesh,
+        in_specs=in_specs,
+        out_specs=out_specs,
+        check_vma=False,
+    )

time: 202 us -> 59.2 us (0.29)
  waiting for transfers between devices: 159 us -> 0 us
  Pallas kernels: 0 us -> 51.3 us
  between operations: 17.1 us -> 3.07 us
  matrix products: 12.8 us -> 0 us
  blocking collectives: 7.88 us -> 0 us
  other arithmetic: 2.9 us -> 0.69 us
    all_gather x5 -> x0, waiting for transfers between devices: 156 us -> none  [the longest x1 37.1 us: shards(): lax.all_gather(value_weight, 'cand', axis=0, tiled=True)]
    pallas_call x0 -> x1, Pallas kernels: none -> 51.3 us  [shards(): pl.pallas_call(functools.partial(kernel, count), out_shape=(jax.ShapeDtyp...]
    dot_general x8 -> x0, matrix products: 12.2 us -> none  [the longest x3 6.15 us: shards(): jnp.dot(columns, piece, preferred_element_type=jnp.float32)]
    all_gather x1 -> x0, blocking collectives: 7.88 us -> none  [shards(): lax.all_gather(token_weight, 'cand', axis=0, tiled=True)]
    unnamed x8, local copies, waits for them, and re-layouts: 0.02 us -> 2.84 us
    unnamed x5 -> x0, waiting for transfers between devices: 2.6 us -> none
  transfers between devices with their start and end apart: 5 -> 0, of which waited for: 5 -> 0; matrix products, arithmetic and copies ran while one was open for 5% -> 0% of each run, Pallas kernels for 0% -> 0%
where the time goes in v1:
time: 59.2 us; the launch traced here: 59.1 us
  Pallas kernels  51.3 us (87%)
  local copies, waits for them, and re-layouts  3.99 us (7%)
  between operations  3.07 us (5%)
  other arithmetic  0.69 us (1%)
    pallas_call x1, Pallas kernels, shards(): pl.pallas_call(functools.partial(kernel, count), out_shape=(jax.ShapeDtyp...  51.3 us
    unnamed x8, local copies, waits for them, and re-layouts  2.84 us

profile of v1, /device:TPU:0, one launch (start us, length us, event | category | flops | bytes accessed | tf_op | source)
XLA Modules:
  0.0 59.1 jit_solution(16558694533336294170)
XLA Ops:
  0.6 0.0 copy-start
  1.3 0.0 copy-start.1
  1.3 0.6 %copy-done.1 = s32[1,128]{1,0:T(1,128)S(1)} copy-done((s32[1,128]{1,0:T(1,128)S(1)}, s32[1,128]{1,0:T(1,128)}, u32[]{:S(2)}) %copy-start.1) | copy-done | bytes 536
  2.0 0.0 copy-done
  2.0 1.1 %gather_fusion = bf16[128]{0:T(256)(128)(2,1)S(1)} fusion(f32[50265]{0:T(1024)S(1)} %copy-done, s32[1024]{0:T(1024)S(1)} %pad_clamp_fusion), kind=kCustom, calls=%fused_computation | custom fusion | bytes 1024 | tf_op jit(solution)/shard_map/jit(_take)/gather | solution.py:354
  3.2 0.7 %broadcast_select_fusion.meta_hbm = f32[8,128]{1,0:T(8,128)} fusion(f32[128]{0:T(128)S(1)} %compare_convert_fusion, f32[128]{0:T(128)S(1)} %fusion.2, pred[8]{0:T(512)(128)(4,1)S(1)} %iota_compare_fusion), kind=kLoop, calls=%fused_computation.3 | loop fusion | flops 1024 | bytes 5128 | tf_op jit(solution)/shard_map/jit(_where)/select_n | solution.py:357
  3.9 51.3 %shard_map.103 = (bf16[128,1024]{1,0:T(8,128)(2,1)}, f32[1,4]{1,0:T(1,128)}, f32[1,1]{1,0:T(1,128)}) custom-call(bf16[128,1024]{1,0:T(8,128)(2,1)} %bitcast.15, f32[8,128]{1,0:T(8,128)} %broadcast_select_fusion.meta_hbm, bf16[256,1024]{1,0:T(8,128)(2,1)} %q_hbm.1, bf16[256,1024]{1,0:T(8,128)(2,1)} %k_hbm.1, bf16[256,1024]{1,0:T(8,128)(2,1)} %v_hbm.1, ...), custom_call_target="tpu_custom_call" | custom-call | tf_op jit(solution)/shard_map/pallas_call | solution.py:361
  55.2 0.0 copy-start.2
  55.2 1.7 %copy.15 = bf16[1,128,1024]{2,1,0:T(8,128)(2,1)} copy(bf16[1,128,1024]{2,1,0:T(8,128)(2,1)} %bitcast.16) | data formatting | bytes 524288
  56.9 0.0 copy-done.2
  56.9 0.5 copy.16
  (5 shorter events, 0.0 us)
Async XLA Ops:
  0.6 1.4 %copy-start = (f32[50265]{0:T(1024)S(1)}, f32[50265]{0:T(1024)}, u32[]{:S(2)}) copy-start(f32[50265]{0:T(1024)} %param.11) | copy-start | bytes 603184
  1.3 0.7 %copy-start.1 = (s32[1,128]{1,0:T(1,128)S(1)}, s32[1,128]{1,0:T(1,128)}, u32[]{:S(2)}) copy-start(s32[1,128]{1,0:T(1,128)} %param.9) | copy-start | bytes 1540
  55.2 1.7 %copy-start.2 = (f32[1,4]{1,0:T(1,128)S(1)}, f32[1,4]{1,0:T(1,128)}, u32[]{:S(2)}) copy-start(f32[1,4]{1,0:T(1,128)} %get-tuple-element.13) | copy-start | bytes 52

commit v2 on v1

--- a/solution.py
+++ b/solution.py
@@ -133,39 +133,38 @@
     k_hbm,
     v_hbm,
     o_hbm,
-    embedded_hbm,
+    embedded_ref,
     utility_ref,
     expected_ref,
     stage,
     full,
-    out_rows,
+    out_full,
     x_all,
     meta,
-    part_out,
-    part_in,
+    context_out,
+    context_full,
     vectors,
     local_sem,
-    w_send,
-    w_recv,
-    f_send,
-    f_recv,
-    x_send,
-    x_recv,
-    m_send,
-    m_recv,
-    p_send,
-    p_recv,
-    e_send,
-    e_recv,
+    send_sem,
+    recv_sem,
 ):
     group, me = lax.axis_index("src"), lax.axis_index("cand")
-    core = lax.rem(group, 2)
+    share = lax.rem(group, 4)
     sibling = (flipped(group, 1), me)
+    mate = (flipped(group, 2), me)
     others = range(1, count)
     peer = [(group, flipped(me, bits)) for bits in range(count)]
     length, width = x_hbm.shape
     rows, columns = stage.shape[1], full.shape[2]
-    half = rows // 2
+    quarter, middle = rows // 4, length // 2
+    started = []
+
+    def push(src_ref, dst_ref, device):
+        number = len(started)
+        copy = remote(src_ref, dst_ref, send_sem.at[number], recv_sem.at[number], device)
+        copy.start()
+        started.append(copy)
+        return copy
 
     def column_block(index):
         return pl.ds(pl.multiple_of(index * columns, columns), columns)
@@ -173,68 +172,102 @@
     def row_block(index):
         return pl.ds(pl.multiple_of(index * rows, rows), rows)
 
-    def row_half(index, which):
-        return pl.ds(pl.multiple_of(index * rows + which * half, half), half)
-
-    own_half = pl.ds(pl.multiple_of(core * half, half), half)
+    def row_share(index, which):
+        return pl.ds(pl.multiple_of(index * rows + which * quarter, quarter), quarter)
+
+    own_share = pl.ds(pl.multiple_of(share * quarter, quarter), quarter)
+    mate_share = lax.rem(share + 2, 4)
 
     weights = (q_hbm, k_hbm, v_hbm)
     loads = [pltpu.make_async_copy(w, stage.at[t], local_sem.at[t]) for t, w in enumerate(weights)]
     loads += [
-        pltpu.make_async_copy(x_hbm, x_all.at[0], local_sem.at[3]),
-        pltpu.make_async_copy(meta_hbm, meta.at[0], local_sem.at[4]),
+        pltpu.make_async_copy(o_hbm, out_full.at[row_block(me), :], local_sem.at[3]),
+        pltpu.make_async_copy(x_hbm, x_all.at[0], local_sem.at[4]),
+        pltpu.make_async_copy(meta_hbm, meta.at[0], local_sem.at[5]),
     ]
     loads += [
         pltpu.make_async_copy(
-            w.at[:, column_block(me)], full.at[t, row_block(me), :], local_sem.at[5 + t]
+            w.at[:, column_block(me)], full.at[t, row_block(me), :], local_sem.at[6 + t]
         )
         for t, w in enumerate(weights)
     ]
-    loads += [pltpu.make_async_copy(o_hbm, out_rows, local_sem.at[8])]
     for load in loads:
         load.start()
 
     barrier = pltpu.get_barrier_semaphore()
-    for target in [sibling] + [peer[r] for r in others]:
+    targets = [sibling, mate] + [peer[r] for r in others]
+    for target in targets:
         pl.semaphore_signal(barrier, inc=1, device_id=target, device_id_type=pl.DeviceIdType.MESH)
-    pl.semaphore_wait(barrier, count)
+    pl.semaphore_wait(barrier, len(targets))
+
+    def exchange(held):
+        part = [held.at[0, pl.ds(0, middle), :], held.at[0, pl.ds(middle, middle), :]]
+
+        def slot(r, which):
+            return held.at[r, pl.ds(which * middle, middle), :]
+
+        first = {1: push(part[0], slot(1, 0), peer[1]), 2: push(part[1], slot(2, 1), peer[2])}
+        second = {1: push(part[1], slot(1, 1), peer[1]), 2: push(part[0], slot(2, 0), peer[2])}
+
+        def relay():
+            first[1].wait_recv()
+            near = push(slot(1, 0), slot(3, 0), peer[2])
+            first[2].wait_recv()
+            return (near, push(slot(2, 1), slot(3, 1), peer[1]))
+
+        return second, relay
 
     for t in range(3):
         loads[t].wait()
-    w_copies, f_copies, x_copies, m_copies = {}, {}, {}, {}
-    for r in others:
-        w_copies[r] = remote(
-            stage.at[:, own_half, column_block(peer[r][1])],
-            full.at[:, row_half(me, core), :],
-            w_send.at[r],
-            w_recv.at[r],
+    w_copies = {}
+    for r in others:
+        w_copies[r] = push(
+            stage.at[:, own_share, column_block(peer[r][1])],
+            full.at[:, row_share(me, share), :],
             peer[r],
         )
-        w_copies[r].start()
-    loads[3].wait()
-    loads[4].wait()
-    for r in others:
-        m_copies[r] = remote(meta.at[0], meta.at[r], m_send.at[r], m_recv.at[r], peer[r])
-        m_copies[r].start()
-    for r in others:
-        x_copies[r] = remote(x_all.at[0], x_all.at[r], x_send.at[r], x_recv.at[r], peer[r])
-        x_copies[r].start()
-    for r in others:
-        w_copies[r].wait_recv()
-        landed = full.at[:, row_half(peer[r][1], core), :]
-        f_copies[r] = remote(landed, landed, f_send.at[r], f_recv.at[r], sibling)
-        f_copies[r].start()
-    for load in loads[5:]:
+    for load in loads[3:6]:
         load.wait()
-    for r in others:
-        f_copies[r].wait_recv()
+    m_copies = {r: push(meta.at[0], meta.at[r], peer[r]) for r in others}
+    o_copies = {
+        r: push(out_full.at[row_share(me, share), :], out_full.at[row_share(me, share), :], peer[r])
+        for r in others
+    }
+    x_second, x_relay = exchange(x_all)
+    for load in loads[6:]:
+        load.wait()
+
+    def spread(copy, landed):
+        copy.wait_recv()
+        return (push(landed, landed, mate), push(landed, landed, sibling))
+
+    def hand_over(copy, landed):
+        copy.wait_recv()
+        return push(landed, landed, sibling)
+
+    def full_share(r, which):
+        return full.at[:, row_share(peer[r][1], which), :]
+
+    def out_share(r, which):
+        return out_full.at[row_share(peer[r][1], which), :]
+
+    w_spread = {r: spread(w_copies[r], full_share(r, share)) for r in others}
+    o_spread = {}
+    o_hand = {}
+    for r in others:
+        o_spread[r] = spread(o_copies[r], out_share(r, share))
+    w_hand = {r: hand_over(w_spread[r][0], full_share(r, mate_share)) for r in others}
+    x_far = x_relay()
+    for r in others:
+        w_spread[r][1].wait_recv()
+        w_hand[r].wait_recv()
 
     lane = lax.broadcasted_iota(jnp.int32, (1, 2 * HEAD), 1)
     scale = 1.0 / math.sqrt(HEAD)
     first = (lane < HEAD).astype(jnp.float32)
     keep = [(first * scale).astype(jnp.bfloat16), ((1.0 - first) * scale).astype(jnp.bfloat16)]
 
-    def partial_of(r):
+    def context_of(r):
         rows_in = x_all[r]
         queries, key_rows, value_rows = tuple(
             jnp.dot(rows_in, full[t], preferred_element_type=jnp.float32).astype(jnp.bfloat16)
@@ -257,41 +290,41 @@
             )
             summed = summed / total
             pieces.append(jnp.where(lane < HEAD, summed[:length], summed[length:]))
-        context = jnp.concatenate(pieces, axis=1).astype(jnp.bfloat16)
-        return jnp.dot(context, out_rows[...], preferred_element_type=jnp.float32)
-
-    mixed = partial_of(0) + x_all[0].astype(jnp.float32)
-    p_copies = {}
-    for r in others:
-        x_copies[r].wait_recv()
+        return jnp.concatenate(pieces, axis=1).astype(jnp.bfloat16)
+
+    context_full[:, column_block(me)] = context_of(0)
+    c_copies = []
+    for r in others:
         m_copies[r].wait_recv()
-        part_out[r] = partial_of(r).astype(jnp.bfloat16)
-        p_copies[r] = remote(part_out.at[r], part_in.at[r], p_send.at[r], p_recv.at[r], peer[r])
-        p_copies[r].start()
-    for r in others:
-        p_copies[r].wait_recv()
-        mixed = mixed + part_in[r].astype(jnp.float32)
+        for copy in ((x_second[r],) if r < 3 else x_far):
+            copy.wait_recv()
+        context_out[r] = context_of(r)
+        c_copies.append(push(context_out.at[r], context_full.at[:, column_block(me)], peer[r]))
+        if r == 2:
+            for q in others:
+                o_hand[q] = hand_over(o_spread[q][0], out_share(q, mate_share))
+    for r in others:
+        o_spread[r][1].wait_recv()
+        o_hand[r].wait_recv()
+    for copy in c_copies:
+        copy.wait_recv()
+
+    mixed = jnp.dot(context_full[...], out_full[...], preferred_element_type=jnp.float32)
+    mixed = mixed + x_all[0].astype(jnp.float32)
     centred = mixed - jnp.mean(mixed, axis=-1, keepdims=True)
     squares = jnp.sum(centred * centred, axis=-1, keepdims=True)
     own = (centred / jnp.sqrt(squares + 0.001)).astype(jnp.bfloat16)
     vectors[0] = own
-    e_copies = {}
-    for r in others:
-        e_copies[r] = remote(vectors.at[0], vectors.at[r], e_send.at[r], e_recv.at[r], peer[r])
-        e_copies[r].start()
-    store = pltpu.make_async_copy(vectors.at[0], embedded_hbm, local_sem.at[0])
+    e_second, e_relay = exchange(vectors)
+    store = pltpu.make_async_copy(vectors.at[0], embedded_ref, local_sem.at[0])
     store.start()
 
     own_weight = meta[0, 0:1, :]
     own_column = jnp.broadcast_to(own_weight, (length, length)).T
     own_total = jnp.sum(own_weight, axis=1, keepdims=True)
     slot = lax.broadcasted_iota(jnp.int32, utility_ref.shape, 1)
-    utility = jnp.zeros(utility_ref.shape, jnp.float32)
-    everything = jnp.zeros((1, 1), jnp.float32)
-    diagonal = None
-    for r in range(count):
-        if r:
-            e_copies[r].wait_recv()
+
+    def pair_of(r):
         far_weight = meta[r, 0:1, :]
         similar = lax.dot_general(
             own, vectors[r], (((1,), (1,)), ((), ())), preferred_element_type=jnp.float32
@@ -302,18 +335,24 @@
         backward = jnp.sum(far_weight * best_own, axis=1, keepdims=True) / jnp.sum(
             far_weight, axis=1, keepdims=True
         )
-        pair = 0.5 * (forward + backward)
+        return 0.5 * (forward + backward)
+
+    diagonal = pair_of(0)
+    e_far = e_relay()
+    utility = jnp.where(slot == me, diagonal, 0.0)
+    everything = diagonal
+    for r in others:
+        for copy in ((e_second[r],) if r < 3 else e_far):
+            copy.wait_recv()
+        pair = pair_of(r)
         utility = jnp.where(slot == peer[r][1], pair, utility)
         everything = everything + pair
-        if r == 0:
-            diagonal = pair
     utility_ref[...] = utility
     expected_ref[...] = (everything - diagonal) / (count - 1)
 
+    for copy in started:
+        copy.wait_send()
     store.wait()
-    for r in others:
-        for copies in (w_copies, f_copies, x_copies, m_copies, p_copies, e_copies):
-            copies[r].wait_send()
 
 
 def shards(
@@ -333,11 +372,10 @@
     columns = width // count
     if (
         local_cands != 1
-        or count < 2
-        or count & (count - 1)
-        or sizes["src"] % 2
+        or count != 4
+        or sizes["src"] % 4
         or columns % (2 * HEAD)
-        or rows % 32
+        or rows % 64
         or length != 128
     ):
         return gathered_shards(
@@ -357,7 +395,7 @@
     meta = jnp.where(row == 0, token_weight, valid)
     anywhere = pl.BlockSpec(memory_space=pl.ANY)
     in_vmem = pl.BlockSpec(memory_space=pltpu.VMEM)
-    pairs = pltpu.SemaphoreType.DMA((count,))
+    copies = pltpu.SemaphoreType.DMA((42,))
     embedded, utility, expected = pl.pallas_call(
         functools.partial(kernel, count),
         out_shape=(
@@ -370,15 +408,16 @@
         scratch_shapes=[
             pltpu.VMEM((3, rows, width), jnp.bfloat16),
             pltpu.VMEM((3, rows * count, columns), jnp.bfloat16),
-            pltpu.VMEM((rows, width), jnp.bfloat16),
+            pltpu.VMEM((rows * count, width), jnp.bfloat16),
             pltpu.VMEM((count, length, width), jnp.bfloat16),
             pltpu.VMEM((count, 8, length), jnp.float32),
-            pltpu.VMEM((count, length, width), jnp.bfloat16),
-            pltpu.VMEM((count, length, width), jnp.bfloat16),
+            pltpu.VMEM((count, length, columns), jnp.bfloat16),
+            pltpu.VMEM((length, width), jnp.bfloat16),
             pltpu.VMEM((count, length, width), jnp.bfloat16),
             pltpu.SemaphoreType.DMA((9,)),
-        ]
-        + [pairs] * 12,
+            copies,
+            copies,
+        ],
         compiler_params=pltpu.CompilerParams(collective_id=0, has_side_effects=True),
     )(
         layer_input.reshape(length, width),

time: 59.2 us -> 48.3 us (0.82)
  Pallas kernels: 51.3 us -> 40.4 us
    pallas_call x1, Pallas kernels: 51.3 us -> 40.4 us  [shards(): pl.pallas_call(functools.partial(kernel, count), out_shape=(jax.ShapeDtyp...]
where the time goes in v2:
time: 48.3 us; the launch traced here: 48.1 us
  Pallas kernels  40.4 us (84%)
  local copies, waits for them, and re-layouts  3.99 us (8%)
  between operations  3.07 us (6%)
  other arithmetic  0.69 us (1%)
    pallas_call x1, Pallas kernels, shards(): pl.pallas_call(functools.partial(kernel, count), out_shape=(jax.ShapeDtyp...  40.4 us
    unnamed x8, local copies, waits for them, and re-layouts  2.84 us
    gather x1, local copies, waits for them, and re-layouts, shards(): token_weight = jnp.take(idf_table, token_ids, axis=0) * valid  1.15 us

profile of v2, /device:TPU:0, one launch (start us, length us, event | category | flops | bytes accessed | tf_op | source)
XLA Modules:
  0.0 48.1 jit_solution(11484581627725838770)
XLA Ops:
  0.6 0.0 copy-start
  1.3 0.0 copy-start.1
  1.3 0.6 %copy-done.1 = s32[1,128]{1,0:T(1,128)S(1)} copy-done((s32[1,128]{1,0:T(1,128)S(1)}, s32[1,128]{1,0:T(1,128)}, u32[]{:S(2)}) %copy-start.1) | copy-done | bytes 536
  2.0 0.0 copy-done
  2.0 1.1 %gather_fusion = bf16[128]{0:T(256)(128)(2,1)S(1)} fusion(f32[50265]{0:T(1024)S(1)} %copy-done, s32[1024]{0:T(1024)S(1)} %pad_clamp_fusion), kind=kCustom, calls=%fused_computation | custom fusion | bytes 1024 | tf_op jit(solution)/shard_map/jit(_take)/gather | solution.py:392
  3.2 0.7 %broadcast_select_fusion.meta_hbm = f32[8,128]{1,0:T(8,128)} fusion(f32[128]{0:T(128)S(1)} %compare_convert_fusion, f32[128]{0:T(128)S(1)} %fusion.2, pred[8]{0:T(512)(128)(4,1)S(1)} %iota_compare_fusion), kind=kLoop, calls=%fused_computation.3 | loop fusion | flops 1024 | bytes 5128 | tf_op jit(solution)/shard_map/jit(_where)/select_n | solution.py:395
  3.9 40.4 %shard_map.103 = (bf16[128,1024]{1,0:T(8,128)(2,1)}, f32[1,4]{1,0:T(1,128)}, f32[1,1]{1,0:T(1,128)}) custom-call(bf16[128,1024]{1,0:T(8,128)(2,1)} %bitcast.15, f32[8,128]{1,0:T(8,128)} %broadcast_select_fusion.meta_hbm, bf16[256,1024]{1,0:T(8,128)(2,1)} %q_hbm.1, bf16[256,1024]{1,0:T(8,128)(2,1)} %k_hbm.1, bf16[256,1024]{1,0:T(8,128)(2,1)} %v_hbm.1, ...), custom_call_target="tpu_custom_call" | custom-call | tf_op jit(solution)/shard_map/pallas_call | solution.py:399
  44.2 0.0 copy-start.2
  44.2 1.7 %copy.15 = bf16[1,128,1024]{2,1,0:T(8,128)(2,1)} copy(bf16[1,128,1024]{2,1,0:T(8,128)(2,1)} %bitcast.16) | data formatting | bytes 524288
  45.9 0.0 copy-done.2
  45.9 0.5 %copy.16 = f32[1,4]{1,0:T(1,128)} copy(f32[1,4]{1,0:T(1,128)S(1)} %copy-done.2) | data formatting | bytes 32
  (5 shorter events, 0.0 us)
Async XLA Ops:
  0.6 1.4 %copy-start = (f32[50265]{0:T(1024)S(1)}, f32[50265]{0:T(1024)}, u32[]{:S(2)}) copy-start(f32[50265]{0:T(1024)} %param.11) | copy-start | bytes 603184
  1.3 0.7 %copy-start.1 = (s32[1,128]{1,0:T(1,128)S(1)}, s32[1,128]{1,0:T(1,128)}, u32[]{:S(2)}) copy-start(s32[1,128]{1,0:T(1,128)} %param.9) | copy-start | bytes 1540
  44.2 1.7 %copy-start.2 = (f32[1,4]{1,0:T(1,128)S(1)}, f32[1,4]{1,0:T(1,128)}, u32[]{:S(2)}) copy-start(f32[1,4]{1,0:T(1,128)} %get-tuple-element.13) | copy-start | bytes 52

commit v3 on v2

--- a/solution.py
+++ b/solution.py
@@ -128,7 +128,9 @@
 def kernel(
     count,
     x_hbm,
-    meta_hbm,
+    ids_hbm,
+    used,
+    table_hbm,
     q_hbm,
     k_hbm,
     v_hbm,
@@ -144,6 +146,8 @@
     context_out,
     context_full,
     vectors,
+    ids,
+    table,
     local_sem,
     send_sem,
     recv_sem,
@@ -183,13 +187,16 @@
     loads += [
         pltpu.make_async_copy(o_hbm, out_full.at[row_block(me), :], local_sem.at[3]),
         pltpu.make_async_copy(x_hbm, x_all.at[0], local_sem.at[4]),
-        pltpu.make_async_copy(meta_hbm, meta.at[0], local_sem.at[5]),
+        pltpu.make_async_copy(ids_hbm, ids, local_sem.at[5]),
     ]
     loads += [
         pltpu.make_async_copy(
             w.at[:, column_block(me)], full.at[t, row_block(me), :], local_sem.at[6 + t]
         )
         for t, w in enumerate(weights)
+    ]
+    loads += [
+        pltpu.make_async_copy(table_hbm, table, local_sem.at[9]),
     ]
     for load in loads:
         load.start()
@@ -228,7 +235,6 @@
         )
     for load in loads[3:6]:
         load.wait()
-    m_copies = {r: push(meta.at[0], meta.at[r], peer[r]) for r in others}
     o_copies = {
         r: push(out_full.at[row_share(me, share), :], out_full.at[row_share(me, share), :], peer[r])
         for r in others
@@ -236,6 +242,17 @@
     x_second, x_relay = exchange(x_all)
     for load in loads[6:]:
         load.wait()
+
+    position = lax.broadcasted_iota(jnp.int32, (1, length), 1)
+
+    def look_up(at, weights_row):
+        return jnp.where(position == at, table[ids[0, at]], weights_row)
+
+    valid_row = (position < used[0]).astype(jnp.float32)
+    weights_row = lax.fori_loop(0, length, look_up, jnp.zeros((1, length), jnp.float32), unroll=8)
+    weights_row = (weights_row * valid_row).astype(jnp.bfloat16).astype(jnp.float32)
+    meta[0] = jnp.concatenate([weights_row, jnp.broadcast_to(valid_row, (7, length))], axis=0)
+    m_copies = {r: push(meta.at[0], meta.at[r], peer[r]) for r in others}
 
     def spread(copy, landed):
         copy.wait_recv()
@@ -316,8 +333,7 @@
     own = (centred / jnp.sqrt(squares + 0.001)).astype(jnp.bfloat16)
     vectors[0] = own
     e_second, e_relay = exchange(vectors)
-    store = pltpu.make_async_copy(vectors.at[0], embedded_ref, local_sem.at[0])
-    store.start()
+    embedded_ref[...] = own
 
     own_weight = meta[0, 0:1, :]
     own_column = jnp.broadcast_to(own_weight, (length, length)).T
@@ -352,7 +368,6 @@
 
     for copy in started:
         copy.wait_send()
-    store.wait()
 
 
 def shards(
@@ -388,23 +403,18 @@
             value_weight,
             output_weight,
         )
-    valid = (jnp.arange(length, dtype=jnp.int32)[None, :] < lengths[:, None]).astype(jnp.float32)
-    token_weight = jnp.take(idf_table, token_ids, axis=0) * valid
-    token_weight = token_weight.astype(jnp.bfloat16).astype(jnp.float32)
-    row = lax.broadcasted_iota(jnp.int32, (8, length), 0)
-    meta = jnp.where(row == 0, token_weight, valid)
     anywhere = pl.BlockSpec(memory_space=pl.ANY)
     in_vmem = pl.BlockSpec(memory_space=pltpu.VMEM)
     copies = pltpu.SemaphoreType.DMA((42,))
     embedded, utility, expected = pl.pallas_call(
         functools.partial(kernel, count),
         out_shape=(
-            jax.ShapeDtypeStruct((length, width), jnp.bfloat16),
-            jax.ShapeDtypeStruct((1, count), jnp.float32),
-            jax.ShapeDtypeStruct((1, 1), jnp.float32),
+            pltpu.VMEM((length, width), jnp.bfloat16),
+            pltpu.VMEM((1, count), jnp.float32),
+            pltpu.VMEM((1, 1), jnp.float32),
         ),
-        in_specs=[anywhere] * 6,
-        out_specs=(anywhere, in_vmem, in_vmem),
+        in_specs=[anywhere] * 2 + [pl.BlockSpec(memory_space=pltpu.SMEM)] + [anywhere] * 5,
+        out_specs=(in_vmem, in_vmem, in_vmem),
         scratch_shapes=[
             pltpu.VMEM((3, rows, width), jnp.bfloat16),
             pltpu.VMEM((3, rows * count, columns), jnp.bfloat16),
@@ -414,14 +424,18 @@
             pltpu.VMEM((count, length, columns), jnp.bfloat16),
             pltpu.VMEM((length, width), jnp.bfloat16),
             pltpu.VMEM((count, length, width), jnp.bfloat16),
-            pltpu.SemaphoreType.DMA((9,)),
+            pltpu.SMEM((1, length), jnp.int32),
+            pltpu.SMEM(idf_table.shape, jnp.float32),
+            pltpu.SemaphoreType.DMA((10,)),
             copies,
             copies,
         ],
         compiler_params=pltpu.CompilerParams(collective_id=0, has_side_effects=True),
     )(
         layer_input.reshape(length, width),
-        meta,
+        token_ids,
+        lengths,
+        idf_table,
         query_weight,
         key_weight,
         value_weight,

time: 48.3 us -> 43.6 us (0.903)
  local copies, waits for them, and re-layouts: 3.99 us -> 1.22 us
  Pallas kernels: 40.4 us -> 39.7 us
  other arithmetic: 0.69 us -> 0 us
  between operations: 3.07 us -> 2.45 us
    unnamed x8 -> x2, local copies, waits for them, and re-layouts: 2.84 us -> 1.22 us
    gather x1 -> x0, local copies, waits for them, and re-layouts: 1.15 us -> none  [shards(): token_weight = jnp.take(idf_table, token_ids, axis=0) * valid]
    select_n x1 -> x0, other arithmetic: 0.66 us -> none  [shards(): meta = jnp.where(row == 0, token_weight, valid)]
    pallas_call x1, Pallas kernels: 40.4 us -> 39.7 us  [shards(): pl.pallas_call(functools.partial(kernel, count), out_shape=(pltpu.VMEM((l...]
where the time goes in v3:
time: 43.6 us; the launch traced here: 43.4 us
  Pallas kernels  39.7 us (91%)
  between operations  2.45 us (6%)
  local copies, waits for them, and re-layouts  1.22 us (3%)
    pallas_call x1, Pallas kernels, shards(): pl.pallas_call(functools.partial(kernel, count), out_shape=(pltpu.VMEM((l...  39.7 us
    unnamed x2, local copies, waits for them, and re-layouts  1.22 us

profile of v3, /device:TPU:0, one launch (start us, length us, event | category | flops | bytes accessed | tf_op | source)
XLA Modules:
  0.0 43.4 jit_solution(624862912436038984)
XLA Ops:
  1.3 39.7 %shard_map.103 = (bf16[128,1024]{1,0:T(8,128)(2,1)S(1)}, f32[1,4]{1,0:T(1,128)S(1)}, f32[1,1]{1,0:T(1,128)S(1)}) custom-call(bf16[128,1024]{1,0:T(8,128)(2,1)} %bitcast.4, s32[1,128]{1,0:T(1,128)} %ids_hbm.1, s32[1]{0:T(128)S(6)} %copy.17.used, f32[50265]{0:T(1024)} %table_hbm.1, bf16[256,1024]{1,0:T(8,128)(2,1)} %q_hbm.1, bf16[256,1024]{1,0:T(8,128)(2,1)} %k_hbm.1, ...), custom_call_target="tpu_custom_call" | custom-call | tf_op jit(solution)/shard_map/pallas_call | solution.py:409
  41.1 0.7 %copy.14 = bf16[1,128,1024]{2,1,0:T(8,128)(2,1)} copy(bf16[1,128,1024]{2,1,0:T(8,128)(2,1)S(1)} %bitcast.3) | data formatting | bytes 524288
  41.8 0.5 %copy.15 = f32[1,4]{1,0:T(1,128)} copy(f32[1,4]{1,0:T(1,128)S(1)} %get-tuple-element.10) | data formatting | bytes 32
